TPU v7x, 32 devices: a whole 2x2x4 slice. The times are simulated.
32 devices in a mesh: grp: 2 (over y), slab: 4 (over z), row: 2 (over x), col: 2 (over core).
Axes of the slice: x: 2, y: 2, z: 4, core: 2. Of those that a mesh axis runs over, the one named last changes fastest.
Arguments:
- image: float32 [3, 64, 32, 256], P(None, ('grp', 'slab'), 'row', 'col'), parts along dimension 1, may hold values from -28 to 28, as said below
- brain_mask: int32 [64, 32, 256], P(('grp', 'slab'), 'row', 'col'), parts along dimension 0, may hold values from 0 to 1, as said below
- labels: int32 [64, 32, 256], P(('grp', 'slab'), 'row', 'col'), parts along dimension 0, may hold values from 0 to 7
Outputs:
- posterior: bfloat16 [8, 64, 32, 256], P(None, ('grp', 'slab'), 'row', 'col'), parts along dimension 1
- bias_field: float32 [3, 64, 32, 256], P(None, ('grp', 'slab'), 'row', 'col'), parts along dimension 1
- class_means: float32 [16, 3], P('grp'), parts along dimension 0
There are 2 independent parts, one for each index of `grp`. A program takes and returns all parts, laid end to end along the dimension named above; each array names one. Nothing has to cross between parts.
Inputs may be any that keep to these rules, and one draw needn't show every extreme that they name: `image`: log intensities of 3 modalities. `brain_mask`: 1 marks a brain cell, 0 a cell outside.
All inputs are finite; a program needn't handle non-finite values.
Results may differ from a plain program's by a relative error of at most 0.001.
Values sent between devices are 32-bit elements; how exact they have to be, the bound alone decides.
No kernel may reach another device: no remote copies, remote signals or barrier semaphores. Data moves between devices by JAX's collectives and lax.ppermute only.
A program may use at most 64 MiB of HBM per device.

v0:
```python
import math
import jax
import jax.numpy as jnp
from jax import lax
from jax.sharding import PartitionSpec as P

M = 3
K = 8
EM_ITERS = 2
MF_PASSES = 2
highest = lax.Precision.HIGHEST
coupling = 1.0
breadth = 8.0


def extended(cells, sides, width):
    for axis, dim in sides:
        count = lax.axis_size(axis)
        ends = count - 1
        head = lax.slice_in_dim(cells, 0, width, axis=dim)
        tail = lax.slice_in_dim(cells, cells.shape[dim] - width, cells.shape[dim], axis=dim)
        cells = jnp.concatenate(
            [
                lax.ppermute(tail, axis, [(i, (i + 1) % count) for i in range(ends)]),
                cells,
                lax.ppermute(head, axis, [((i + 1) % count, i) for i in range(ends)]),
            ],
            axis=dim,
        )
    return cells


def circulant(length):
    index = jnp.arange(length, dtype=jnp.int32)
    folded = jnp.minimum(index, length - index).astype(jnp.float32) / length
    response = jnp.exp(-2.0 * math.pi**2 * (length / breadth) ** 2 * folded * folded)
    product = index[:, None] * index[None, :] % length
    angles = 2.0 * math.pi / length * product.astype(jnp.float32)
    cosine = jnp.cos(angles)
    sine = jnp.sin(angles)
    even_part = jnp.dot(cosine * response[None, :], cosine.T, precision=highest)
    odd_part = jnp.dot(sine * response[None, :], sine.T, precision=highest)
    return (even_part + odd_part) / length


def neighbour_sum(belief):
    padded = extended(belief, (("slab", 1), ("row", 2), ("col", 3)), 1)
    total = padded[:, 2:, 1:-1, 1:-1] + padded[:, :-2, 1:-1, 1:-1]
    total = total + padded[:, 1:-1, 2:, 1:-1] + padded[:, 1:-1, :-2, 1:-1]
    total = total + padded[:, 1:-1, 1:-1, 2:] + padded[:, 1:-1, 1:-1, :-2]
    return total


def class_moments(belief, corrected):
    flat = belief.reshape(K, -1)
    values = corrected.reshape(M, -1)
    count, first, squares = lax.psum(
        (
            jnp.sum(flat, axis=1),
            jnp.dot(flat, values.T, precision=highest),
            jnp.dot(flat, (values * values).T, precision=highest),
        ),
        ("slab", "row", "col"),
    )
    means = first / (count + 1.0)[:, None]
    spread = squares - 2.0 * means * first + means * means * count[:, None]
    variance = (spread + 1.0) / (count + 1.0)[:, None]
    return (count, means, variance)


def log_density(corrected, means, variance, prior):
    offset = corrected[None] - means[:, :, None, None, None]
    terms = (
        offset * offset / variance[:, :, None, None, None]
        + jnp.log(variance)[:, :, None, None, None]
    )
    return jnp.log(prior)[:, None, None, None] - 0.5 * jnp.sum(terms, axis=1)


def smoothed(residual, column_local, row_table, slab_table):
    across = jnp.einsum(
        "msrc,cd->msrd",
        lax.all_gather(residual, "col", axis=3, tiled=True),
        column_local,
        precision=highest,
    )
    mixed = jnp.einsum(
        "msrc,rq->msqc",
        lax.all_to_all(across, "row", split_axis=1, concat_axis=2, tiled=True),
        row_table,
        precision=highest,
    )
    across = lax.all_to_all(mixed, "row", split_axis=2, concat_axis=1, tiled=True)
    mixed = jnp.einsum(
        "msrc,sq->mqrc",
        lax.all_to_all(across, "slab", split_axis=2, concat_axis=1, tiled=True),
        slab_table,
        precision=highest,
    )
    return lax.all_to_all(mixed, "slab", split_axis=1, concat_axis=2, tiled=True)


def local(image, brain_mask, labels):
    channels, slabs, rows, columns = image.shape
    inside = brain_mask.astype(jnp.float32)
    kinds = jnp.arange(K, dtype=jnp.int32)
    belief = (labels[None] == kinds[:, None, None, None]).astype(jnp.float32) * inside[None]
    column_table = circulant(columns * lax.axis_size("col"))
    column_local = lax.dynamic_slice_in_dim(
        column_table, lax.axis_index("col") * columns, columns, 1
    )
    row_table = circulant(rows * lax.axis_size("row"))
    slab_table = circulant(slabs * lax.axis_size("slab"))
    bias_field = jnp.zeros_like(image)
    means = jnp.zeros((K, channels), jnp.float32)
    for iteration in range(EM_ITERS):
        corrected = image - bias_field
        count, means, variance = class_moments(belief, corrected)
        prior = (count + 1.0) / (jnp.sum(count) + K)
        total = jnp.sum(belief, axis=0)
        removed = jnp.dot(means.T, belief.reshape(K, -1), precision=highest).reshape(image.shape)
        residual = image * total[None] - removed
        bias_field = smoothed(residual, column_local, row_table, slab_table)
        corrected = image - bias_field
        density = log_density(corrected, means, variance, prior)
        for sweep_index in range(MF_PASSES):
            belief = (
                jax.nn.softmax(density + coupling * neighbour_sum(belief), axis=0) * inside[None]
            )
    return (belief.astype(jnp.bfloat16), bias_field, means)


def solution(mesh):
    placed = (
        P(None, ("grp", "slab"), "row", "col"),
        P(("grp", "slab"), "row", "col"),
        P(("grp", "slab"), "row", "col"),
    )
    return jax.shard_map(
        local,
        mesh=mesh,
        in_specs=placed,
        out_specs=(
            P(None, ("grp", "slab"), "row", "col"),
            P(None, ("grp", "slab"), "row", "col"),
            P("grp", None),
        ),
        check_vma=False,
    )
```

profile of v0, /device:TPU:0, one launch (start us, length us, event | category | flops | bytes accessed | tf_op | source)
XLA Modules:
  0.0 240.7 jit_solution(11587355852781525625)
XLA Ops:
  6.4 35.4 %all-reduce.1 = (f32[8,3]{0,1:T(4,128)S(1)}, f32[8,3]{0,1:T(4,128)S(1)}, f32[8]{0:T(128)S(1)}) all-reduce(f32[8,3]{0,1:T(4,128)S(1)} %fusion.2, f32[8,3]{0,1:T(4,128)S(1)} %convolution_bitcast_fusion.6, f32[8]{0:T(128)S(1)} %select_reduce_fusion), channel_id=1, replica_groups=mesh['grp'=2,'slab'=4,'row'=2,'col'=2] {'slab','row','col'}, use_global_device_ids=true, to_apply=%region_5.6 | all-reduce | flops 56 | bytes 448 | tf_op jit(solution)/shard_map/psum | solution.py:57
  44.3 2.2 all_gather.6
  47.7 3.4 %all-to-all-start = ((f32[3,8,16,128]{3,2,0,1:T(8,128)}), f32[3,8,16,128]{3,2,0,1:T(8,128)S(1)}, u32[]{:S(2)}, u32[]{:S(2)}) async-start(f32[3,8,16,128]{3,2,0,1:T(8,128)} %fusion.39), calls=%async_computation | async-start | bytes 393216 | tf_op jit(solution)/shard_map/all_to_all | solution.py:89
  51.6 4.5 %all-to-all-done = f32[3,8,16,128]{3,2,0,1:T(8,128)S(1)} async-done(((f32[3,8,16,128]{3,2,0,1:T(8,128)}), f32[3,8,16,128]{3,2,0,1:T(8,128)S(1)}, u32[]{:S(2)}, u32[]{:S(2)}) %all-to-all-start) | async-done | bytes 196640 | tf_op jit(solution)/shard_map/all_to_all | solution.py:89
  57.3 3.4 %all-to-all-start.1 = ((f32[3,4,32,128]{3,1,0,2:T(4,128)}), f32[3,4,32,128]{3,1,0,2:T(4,128)S(1)}, u32[]{:S(2)}, u32[]{:S(2)}) async-start(f32[3,4,32,128]{3,1,0,2:T(4,128)} %copy.240), calls=%async_computation.1 | async-start | bytes 393216 | tf_op jit(solution)/shard_map/all_to_all | solution.py:93
  66.4 3.4 %all-to-all-start.2 = ((f32[3,8,16,128]{3,1,0,2:T(8,128)}), f32[3,8,16,128]{3,1,0,2:T(8,128)S(1)}, u32[]{:S(2)}, u32[]{:S(2)}) async-start(f32[3,8,16,128]{3,1,0,2:T(8,128)} %copy.243), calls=%async_computation.2 | async-start | bytes 393216 | tf_op jit(solution)/shard_map/all_to_all | solution.py:96
  71.2 4.5 %collective-permute-start.3 = (f32[8,10,1,128]{3,0,2,1:T(8,128)S(1)}, f32[8,10,1,128]{3,0,2,1:T(8,128)S(1)}, u32[]{:S(2)}, u32[]{:S(2)}) collective-permute-start(f32[8,10,1,128]{3,0,2,1:T(8,128)S(1)} %copy.339), channel_id=1, source_target_pairs={{0,2},{1,3},{4,6},{5,7},{8,10},{9,11},{12,14},{13,15},{16,18},{17,... | collective-permute-start | bytes 122888 | tf_op jit(solution)/shard_map/ppermute | solution.py:24
  78.8 5.0 %all-to-all-start.3 = ((f32[3,32,4,128]{3,2,0,1:T(4,128)}), f32[3,32,4,128]{3,2,0,1:T(4,128)S(1)}, u32[]{:S(2)}, u32[]{:S(2)}) async-start(f32[3,32,4,128]{3,2,0,1:T(4,128)} %copy.247), calls=%async_computation.3 | async-start | bytes 393216 | tf_op jit(solution)/shard_map/all_to_all | solution.py:100
  96.2 3.9 %collective-permute-start.7 = (f32[8,1,16,128]{3,2,1,0:T(8,128)S(1)}, f32[8,1,16,128]{3,2,1,0:T(8,128)S(1)}, u32[]{:S(2)}, u32[]{:S(2)}) collective-permute-start(f32[8,1,16,128]{3,2,1,0:T(8,128)S(1)} %get-tuple-element.53), channel_id=1, source_target_pairs={{0,4},{4,8},{8,12},{1,5},{5,9},{9,13},{2,6},{6,10},{10,14},{3,7},{... | collective-permute-start | bytes 196616 | tf_op jit(solution)/shard_map/ppermute | solution.py:24
  102.0 4.3 %collective-permute-done.6 = f32[8,1,16,128]{3,2,1,0:T(8,128)S(1)} collective-permute-done((f32[8,1,16,128]{3,2,1,0:T(8,128)S(1)}, f32[8,1,16,128]{3,2,1,0:T(8,128)S(1)}, u32[]{:S(2)}, u32[]{:S(2)}) %collective-permute-start.6) | collective-permute-done | bytes 65568 | tf_op jit(solution)/shard_map/ppermute | solution.py:26
  107.7 4.7 %collective-permute-start.9 = (f32[8,10,1,128]{3,0,2,1:T(8,128)S(1)}, f32[8,10,1,128]{3,0,2,1:T(8,128)S(1)}, u32[]{:S(2)}, u32[]{:S(2)}) collective-permute-start(f32[8,10,1,128]{3,0,2,1:T(8,128)S(1)} %copy.341), channel_id=1, source_target_pairs={{0,2},{1,3},{4,6},{5,7},{8,10},{9,11},{12,14},{13,15},{16,18},{17,... | collective-permute-start | bytes 122888 | tf_op jit(solution)/shard_map/ppermute | solution.py:24
  118.1 3.8 %collective-permute-start.11 = (f32[8,10,18,1]{2,0,3,1:T(8,128)S(1)}, f32[8,10,18,1]{2,0,3,1:T(8,128)}, u32[]{:S(2)}, u32[]{:S(2)}) collective-permute-start(f32[8,10,18,1]{2,0,3,1:T(8,128)S(1)} %copy.270), channel_id=1, source_target_pairs={{0,1},{2,3},{4,5},{6,7},{8,9},{10,11},{12,13},{14,15},{16,17},{18,... | collective-permute-start | bytes 17288 | tf_op jit(solution)/shard_map/ppermute | solution.py:24
  128.4 32.9 %all-reduce = (f32[8,3]{0,1:T(4,128)S(1)}, f32[8]{0:T(128)S(1)}, f32[8,3]{0,1:T(4,128)S(1)}) all-reduce(f32[8,3]{0,1:T(4,128)S(1)} %convolution_bitcast_fusion.5, f32[8]{0:T(128)S(1)} %get-tuple-element.10, f32[8,3]{0,1:T(4,128)S(1)} %convolution_bitcast_fusion.4), channel_id=1, replica_groups=mesh['grp'=2,'slab'=4,'row'=2,'col'=2] {'slab','row','col'}, use_global_device_ids=true, to_apply=%region_15.16 | all-reduce | flops 56 | bytes 448 | tf_op jit(solution)/shard_map/psum | solution.py:57
  163.6 2.2 all_gather.7
  166.3 7.4 %all_to_all.144 = f32[3,8,16,128]{3,2,0,1:T(8,128)S(1)} all-to-all(f32[3,8,16,128]{3,2,0,1:T(8,128)S(1)} %fusion.37), channel_id=1, replica_groups=mesh['grp'=2,'slab'=4,'row'=2,'col'=2] {'row'}, dimensions={1} | all-to-all | bytes 393216 | tf_op jit(solution)/shard_map/all_to_all | solution.py:89
  175.0 3.4 %all-to-all-start.5 = ((f32[3,4,32,128]{3,1,0,2:T(4,128)}), f32[3,4,32,128]{3,1,0,2:T(4,128)S(1)}, u32[]{:S(2)}, u32[]{:S(2)}) async-start(f32[3,4,32,128]{3,1,0,2:T(4,128)} %copy.281), calls=%async_computation.5 | async-start | bytes 393216 | tf_op jit(solution)/shard_map/all_to_all | solution.py:93
  184.0 3.4 %all-to-all-start.6 = ((f32[3,8,16,128]{3,1,0,2:T(8,128)}), f32[3,8,16,128]{3,1,0,2:T(8,128)S(1)}, u32[]{:S(2)}, u32[]{:S(2)}) async-start(f32[3,8,16,128]{3,1,0,2:T(8,128)} %copy.284), calls=%async_computation.6 | async-start | bytes 393216 | tf_op jit(solution)/shard_map/all_to_all | solution.py:96
  188.8 4.5 %collective-permute-start.15 = (f32[8,10,1,128]{3,0,2,1:T(8,128)S(1)}, f32[8,10,1,128]{3,0,2,1:T(8,128)S(1)}, u32[]{:S(2)}, u32[]{:S(2)}) collective-permute-start(f32[8,10,1,128]{3,0,2,1:T(8,128)S(1)} %copy.343), channel_id=1, source_target_pairs={{0,2},{1,3},{4,6},{5,7},{8,10},{9,11},{12,14},{13,15},{16,18},{17,... | collective-permute-start | bytes 122888 | tf_op jit(solution)/shard_map/ppermute | solution.py:24
  196.4 5.0 %all-to-all-start.7 = ((f32[3,32,4,128]{3,2,0,1:T(4,128)}), f32[3,32,4,128]{3,2,0,1:T(4,128)S(1)}, u32[]{:S(2)}, u32[]{:S(2)}) async-start(f32[3,32,4,128]{3,2,0,1:T(4,128)} %copy.288), calls=%async_computation.7 | async-start | bytes 393216 | tf_op jit(solution)/shard_map/all_to_all | solution.py:100
  206.3 3.0 %collective-permute-start.17 = (f32[8,10,18,1]{2,0,3,1:T(8,128)S(1)}, f32[8,10,18,1]{2,0,3,1:T(8,128)S(1)}, u32[]{:S(2)}, u32[]{:S(2)}) collective-permute-start(f32[8,10,18,1]{2,0,3,1:T(8,128)S(1)} %copy.303), channel_id=1, source_target_pairs={{0,1},{2,3},{4,5},{6,7},{8,9},{10,11},{12,13},{14,15},{16,17},{18,... | collective-permute-start | bytes 17288 | tf_op jit(solution)/shard_map/ppermute | solution.py:24
  214.0 3.9 %collective-permute-start.19 = (f32[8,1,16,128]{3,2,1,0:T(8,128)S(1)}, f32[8,1,16,128]{3,2,1,0:T(8,128)S(1)}, u32[]{:S(2)}, u32[]{:S(2)}) collective-permute-start(f32[8,1,16,128]{3,2,1,0:T(8,128)S(1)} %get-tuple-element.49), channel_id=1, source_target_pairs={{0,4},{4,8},{8,12},{1,5},{5,9},{9,13},{2,6},{6,10},{10,14},{3,7},{... | collective-permute-start | bytes 196616 | tf_op jit(solution)/shard_map/ppermute | solution.py:24
  219.8 4.3 %collective-permute-done.18 = f32[8,1,16,128]{3,2,1,0:T(8,128)S(1)} collective-permute-done((f32[8,1,16,128]{3,2,1,0:T(8,128)S(1)}, f32[8,1,16,128]{3,2,1,0:T(8,128)S(1)}, u32[]{:S(2)}, u32[]{:S(2)}) %collective-permute-start.18) | collective-permute-done | bytes 65568 | tf_op jit(solution)/shard_map/ppermute | solution.py:26
  225.5 4.8 %collective-permute-start.21 = (f32[8,10,1,128]{3,0,2,1:T(8,128)S(1)}, f32[8,10,1,128]{3,0,2,1:T(8,128)S(1)}, u32[]{:S(2)}, u32[]{:S(2)}) collective-permute-start(f32[8,10,1,128]{3,0,2,1:T(8,128)S(1)} %copy.345), channel_id=1, source_target_pairs={{0,2},{1,3},{4,6},{5,7},{8,10},{9,11},{12,14},{13,15},{16,18},{17,... | collective-permute-start | bytes 122888 | tf_op jit(solution)/shard_map/ppermute | solution.py:24
  234.6 3.0 %collective-permute-start.23 = (f32[8,10,18,1]{2,0,3,1:T(8,128)S(1)}, f32[8,10,18,1]{2,0,3,1:T(8,128)S(1)}, u32[]{:S(2)}, u32[]{:S(2)}) collective-permute-start(f32[8,10,18,1]{2,0,3,1:T(8,128)S(1)} %copy.313), channel_id=1, source_target_pairs={{0,1},{2,3},{4,5},{6,7},{8,9},{10,11},{12,13},{14,15},{16,17},{18,... | collective-permute-start | bytes 17288 | tf_op jit(solution)/shard_map/ppermute | solution.py:24
  (194 shorter events, 81.2 us)
Async XLA Ops:
  47.7 8.5 %all-to-all-start = ((f32[3,8,16,128]{3,2,0,1:T(8,128)}), f32[3,8,16,128]{3,2,0,1:T(8,128)S(1)}, u32[]{:S(2)}, u32[]{:S(2)}) async-start(f32[3,8,16,128]{3,2,0,1:T(8,128)} %fusion.39), calls=%async_computation | async-start | bytes 393216 | tf_op jit(solution)/shard_map/all_to_all | solution.py:89
  57.3 8.2 %all-to-all-start.1 = ((f32[3,4,32,128]{3,1,0,2:T(4,128)}), f32[3,4,32,128]{3,1,0,2:T(4,128)S(1)}, u32[]{:S(2)}, u32[]{:S(2)}) async-start(f32[3,4,32,128]{3,1,0,2:T(4,128)} %copy.240), calls=%async_computation.1 | async-start | bytes 393216 | tf_op jit(solution)/shard_map/all_to_all | solution.py:93
  60.8 8.9 %collective-permute-start.1 = (f32[8,1,16,128]{3,2,1,0:T(8,128)S(1)}, f32[8,1,16,128]{3,2,1,0:T(8,128)S(1)}, u32[]{:S(2)}, u32[]{:S(2)}) collective-permute-start(f32[8,1,16,128]{3,2,1,0:T(8,128)S(1)} %get-tuple-element.55), channel_id=1, source_target_pairs={{0,4},{4,8},{8,12},{1,5},{5,9},{9,13},{2,6},{6,10},{10,14},{3,7},{... | collective-permute-start | bytes 196616 | tf_op jit(solution)/shard_map/ppermute | solution.py:24
  62.1 7.7 %collective-permute-start = (f32[8,1,16,128]{3,2,1,0:T(8,128)S(1)}, f32[8,1,16,128]{3,2,1,0:T(8,128)S(1)}, u32[]{:S(2)}, u32[]{:S(2)}) collective-permute-start(f32[8,1,16,128]{3,2,1,0:T(8,128)S(1)} %get-tuple-element.56), channel_id=1, source_target_pairs={{4,0},{8,4},{12,8},{5,1},{9,5},{13,9},{6,2},{10,6},{14,10},{7,3},{... | collective-permute-start | bytes 196616 | tf_op jit(solution)/shard_map/ppermute | solution.py:26
  66.4 11.2 %all-to-all-start.2 = ((f32[3,8,16,128]{3,1,0,2:T(8,128)}), f32[3,8,16,128]{3,1,0,2:T(8,128)S(1)}, u32[]{:S(2)}, u32[]{:S(2)}) async-start(f32[3,8,16,128]{3,1,0,2:T(8,128)} %copy.243), calls=%async_computation.2 | async-start | bytes 393216 | tf_op jit(solution)/shard_map/all_to_all | solution.py:96
  69.8 5.9 %collective-permute-start.2 = (f32[8,10,1,128]{3,0,2,1:T(8,128)S(1)}, f32[8,10,1,128]{3,0,2,1:T(8,128)S(1)}, u32[]{:S(2)}, u32[]{:S(2)}) collective-permute-start(f32[8,10,1,128]{3,0,2,1:T(8,128)S(1)} %copy.338), channel_id=1, source_target_pairs={{2,0},{3,1},{6,4},{7,5},{10,8},{11,9},{14,12},{15,13},{18,16},{19,... | collective-permute-start | bytes 122888 | tf_op jit(solution)/shard_map/ppermute | solution.py:26
  71.2 6.2 %collective-permute-start.3 = (f32[8,10,1,128]{3,0,2,1:T(8,128)S(1)}, f32[8,10,1,128]{3,0,2,1:T(8,128)S(1)}, u32[]{:S(2)}, u32[]{:S(2)}) collective-permute-start(f32[8,10,1,128]{3,0,2,1:T(8,128)S(1)} %copy.339), channel_id=1, source_target_pairs={{0,2},{1,3},{4,6},{5,7},{8,10},{9,11},{12,14},{13,15},{16,18},{17,... | collective-permute-start | bytes 122888 | tf_op jit(solution)/shard_map/ppermute | solution.py:24
  78.8 15.2 %all-to-all-start.3 = ((f32[3,32,4,128]{3,2,0,1:T(4,128)}), f32[3,32,4,128]{3,2,0,1:T(4,128)S(1)}, u32[]{:S(2)}, u32[]{:S(2)}) async-start(f32[3,32,4,128]{3,2,0,1:T(4,128)} %copy.247), calls=%async_computation.3 | async-start | bytes 393216 | tf_op jit(solution)/shard_map/all_to_all | solution.py:100
  96.2 5.8 %collective-permute-start.7 = (f32[8,1,16,128]{3,2,1,0:T(8,128)S(1)}, f32[8,1,16,128]{3,2,1,0:T(8,128)S(1)}, u32[]{:S(2)}, u32[]{:S(2)}) collective-permute-start(f32[8,1,16,128]{3,2,1,0:T(8,128)S(1)} %get-tuple-element.53), channel_id=1, source_target_pairs={{0,4},{4,8},{8,12},{1,5},{5,9},{9,13},{2,6},{6,10},{10,14},{3,7},{... | collective-permute-start | bytes 196616 | tf_op jit(solution)/shard_map/ppermute | solution.py:24
  100.1 6.2 %collective-permute-start.6 = (f32[8,1,16,128]{3,2,1,0:T(8,128)S(1)}, f32[8,1,16,128]{3,2,1,0:T(8,128)S(1)}, u32[]{:S(2)}, u32[]{:S(2)}) collective-permute-start(f32[8,1,16,128]{3,2,1,0:T(8,128)S(1)} %get-tuple-element.54), channel_id=1, source_target_pairs={{4,0},{8,4},{12,8},{5,1},{9,5},{13,9},{6,2},{10,6},{14,10},{7,3},{... | collective-permute-start | bytes 196616 | tf_op jit(solution)/shard_map/ppermute | solution.py:26
  106.4 6.0 %collective-permute-start.8 = (f32[8,10,1,128]{3,0,2,1:T(8,128)S(1)}, f32[8,10,1,128]{3,0,2,1:T(8,128)S(1)}, u32[]{:S(2)}, u32[]{:S(2)}) collective-permute-start(f32[8,10,1,128]{3,0,2,1:T(8,128)S(1)} %copy.340), channel_id=1, source_target_pairs={{2,0},{3,1},{6,4},{7,5},{10,8},{11,9},{14,12},{15,13},{18,16},{19,... | collective-permute-start | bytes 122888 | tf_op jit(solution)/shard_map/ppermute | solution.py:26
  107.7 6.2 %collective-permute-start.9 = (f32[8,10,1,128]{3,0,2,1:T(8,128)S(1)}, f32[8,10,1,128]{3,0,2,1:T(8,128)S(1)}, u32[]{:S(2)}, u32[]{:S(2)}) collective-permute-start(f32[8,10,1,128]{3,0,2,1:T(8,128)S(1)} %copy.341), channel_id=1, source_target_pairs={{0,2},{1,3},{4,6},{5,7},{8,10},{9,11},{12,14},{13,15},{16,18},{17,... | collective-permute-start | bytes 122888 | tf_op jit(solution)/shard_map/ppermute | solution.py:24
  116.2 5.6 %collective-permute-start.10 = (f32[8,10,18,1]{2,0,3,1:T(8,128)}, f32[8,10,18,1]{2,0,3,1:T(8,128)S(1)}, u32[]{:S(2)}, u32[]{:S(2)}) collective-permute-start(f32[8,10,18,1]{2,0,3,1:T(8,128)} %copy.268), channel_id=1, source_target_pairs={{1,0},{3,2},{5,4},{7,6},{9,8},{11,10},{13,12},{15,14},{17,16},{19,... | collective-permute-start | bytes 17288 | tf_op jit(solution)/shard_map/ppermute | solution.py:26
  175.0 8.2 %all-to-all-start.5 = ((f32[3,4,32,128]{3,1,0,2:T(4,128)}), f32[3,4,32,128]{3,1,0,2:T(4,128)S(1)}, u32[]{:S(2)}, u32[]{:S(2)}) async-start(f32[3,4,32,128]{3,1,0,2:T(4,128)} %copy.281), calls=%async_computation.5 | async-start | bytes 393216 | tf_op jit(solution)/shard_map/all_to_all | solution.py:93
  178.4 8.9 %collective-permute-start.13 = (f32[8,1,16,128]{3,2,1,0:T(8,128)S(1)}, f32[8,1,16,128]{3,2,1,0:T(8,128)S(1)}, u32[]{:S(2)}, u32[]{:S(2)}) collective-permute-start(f32[8,1,16,128]{3,2,1,0:T(8,128)S(1)} %get-tuple-element.51), channel_id=1, source_target_pairs={{0,4},{4,8},{8,12},{1,5},{5,9},{9,13},{2,6},{6,10},{10,14},{3,7},{... | collective-permute-start | bytes 196616 | tf_op jit(solution)/shard_map/ppermute | solution.py:24
  179.7 7.7 %collective-permute-start.12 = (f32[8,1,16,128]{3,2,1,0:T(8,128)S(1)}, f32[8,1,16,128]{3,2,1,0:T(8,128)S(1)}, u32[]{:S(2)}, u32[]{:S(2)}) collective-permute-start(f32[8,1,16,128]{3,2,1,0:T(8,128)S(1)} %get-tuple-element.52), channel_id=1, source_target_pairs={{4,0},{8,4},{12,8},{5,1},{9,5},{13,9},{6,2},{10,6},{14,10},{7,3},{... | collective-permute-start | bytes 196616 | tf_op jit(solution)/shard_map/ppermute | solution.py:26
  184.0 11.2 %all-to-all-start.6 = ((f32[3,8,16,128]{3,1,0,2:T(8,128)}), f32[3,8,16,128]{3,1,0,2:T(8,128)S(1)}, u32[]{:S(2)}, u32[]{:S(2)}) async-start(f32[3,8,16,128]{3,1,0,2:T(8,128)} %copy.284), calls=%async_computation.6 | async-start | bytes 393216 | tf_op jit(solution)/shard_map/all_to_all | solution.py:96
  187.5 5.9 %collective-permute-start.14 = (f32[8,10,1,128]{3,0,2,1:T(8,128)S(1)}, f32[8,10,1,128]{3,0,2,1:T(8,128)S(1)}, u32[]{:S(2)}, u32[]{:S(2)}) collective-permute-start(f32[8,10,1,128]{3,0,2,1:T(8,128)S(1)} %copy.342), channel_id=1, source_target_pairs={{2,0},{3,1},{6,4},{7,5},{10,8},{11,9},{14,12},{15,13},{18,16},{19,... | collective-permute-start | bytes 122888 | tf_op jit(solution)/shard_map/ppermute | solution.py:26
  188.8 6.2 %collective-permute-start.15 = (f32[8,10,1,128]{3,0,2,1:T(8,128)S(1)}, f32[8,10,1,128]{3,0,2,1:T(8,128)S(1)}, u32[]{:S(2)}, u32[]{:S(2)}) collective-permute-start(f32[8,10,1,128]{3,0,2,1:T(8,128)S(1)} %copy.343), channel_id=1, source_target_pairs={{0,2},{1,3},{4,6},{5,7},{8,10},{9,11},{12,14},{13,15},{16,18},{17,... | collective-permute-start | bytes 122888 | tf_op jit(solution)/shard_map/ppermute | solution.py:24
  196.4 15.4 %all-to-all-start.7 = ((f32[3,32,4,128]{3,2,0,1:T(4,128)}), f32[3,32,4,128]{3,2,0,1:T(4,128)S(1)}, u32[]{:S(2)}, u32[]{:S(2)}) async-start(f32[3,32,4,128]{3,2,0,1:T(4,128)} %copy.288), calls=%async_computation.7 | async-start | bytes 393216 | tf_op jit(solution)/shard_map/all_to_all | solution.py:100
  214.0 5.8 %collective-permute-start.19 = (f32[8,1,16,128]{3,2,1,0:T(8,128)S(1)}, f32[8,1,16,128]{3,2,1,0:T(8,128)S(1)}, u32[]{:S(2)}, u32[]{:S(2)}) collective-permute-start(f32[8,1,16,128]{3,2,1,0:T(8,128)S(1)} %get-tuple-element.49), channel_id=1, source_target_pairs={{0,4},{4,8},{8,12},{1,5},{5,9},{9,13},{2,6},{6,10},{10,14},{3,7},{... | collective-permute-start | bytes 196616 | tf_op jit(solution)/shard_map/ppermute | solution.py:24
  217.9 6.2 %collective-permute-start.18 = (f32[8,1,16,128]{3,2,1,0:T(8,128)S(1)}, f32[8,1,16,128]{3,2,1,0:T(8,128)S(1)}, u32[]{:S(2)}, u32[]{:S(2)}) collective-permute-start(f32[8,1,16,128]{3,2,1,0:T(8,128)S(1)} %get-tuple-element.50), channel_id=1, source_target_pairs={{4,0},{8,4},{12,8},{5,1},{9,5},{13,9},{6,2},{10,6},{14,10},{7,3},{... | collective-permute-start | bytes 196616 | tf_op jit(solution)/shard_map/ppermute | solution.py:26
  224.1 6.1 %collective-permute-start.20 = (f32[8,10,1,128]{3,0,2,1:T(8,128)S(1)}, f32[8,10,1,128]{3,0,2,1:T(8,128)S(1)}, u32[]{:S(2)}, u32[]{:S(2)}) collective-permute-start(f32[8,10,1,128]{3,0,2,1:T(8,128)S(1)} %copy.344), channel_id=1, source_target_pairs={{2,0},{3,1},{6,4},{7,5},{10,8},{11,9},{14,12},{15,13},{18,16},{19,... | collective-permute-start | bytes 122888 | tf_op jit(solution)/shard_map/ppermute | solution.py:26
  225.5 6.2 %collective-permute-start.21 = (f32[8,10,1,128]{3,0,2,1:T(8,128)S(1)}, f32[8,10,1,128]{3,0,2,1:T(8,128)S(1)}, u32[]{:S(2)}, u32[]{:S(2)}) collective-permute-start(f32[8,10,1,128]{3,0,2,1:T(8,128)S(1)} %copy.345), channel_id=1, source_target_pairs={{0,2},{1,3},{4,6},{5,7},{8,10},{9,11},{12,14},{13,15},{16,18},{17,... | collective-permute-start | bytes 122888 | tf_op jit(solution)/shard_map/ppermute | solution.py:24
  (26 other events, 231.1 us)
where the time goes:
time: 242 us; the launch traced here: 241 us
  starting transfers between devices  82.7 us (34%)
  blocking collectives  80.2 us (33%)
  waiting for transfers between devices  26.4 us (11%)
  local copies, waits for them, and re-layouts  26 us (11%)
  matrix products  12.9 us (5%)
  other arithmetic  9.53 us (4%)
  between operations  2.89 us (1%)
    psum x2, blocking collectives, class_moments(): lax.psum((jnp.sum(flat, axis=1), jnp.dot(flat, values.T, precision=highes...  68.3 us
    ppermute x12, starting transfers between devices, extended(): lax.ppermute(tail, axis, [(i, (i + 1) % count) for i in range(ends)])  40.1 us
    ppermute x12, starting transfers between devices, extended(): lax.ppermute(head, axis, [((i + 1) % count, i) for i in range(ends)])  15.5 us
    ppermute x12, waiting for transfers between devices, extended(): lax.ppermute(head, axis, [((i + 1) % count, i) for i in range(ends)])  10.2 us
    all_to_all x2, starting transfers between devices, smoothed(): lax.all_to_all(mixed, 'slab', split_axis=1, concat_axis=2, tiled=True)  10.1 us
    slice x8, local copies, waits for them, and re-layouts, extended(): head = lax.slice_in_dim(cells, 0, width, axis=dim)  8.48 us
    all_to_all x1, blocking collectives, smoothed(): lax.all_to_all(across, 'row', split_axis=1, concat_axis=2, tiled=True)  7.42 us
    ppermute x12, waiting for transfers between devices, extended(): lax.ppermute(tail, axis, [(i, (i + 1) % count) for i in range(ends)])  7.35 us
  transfers between devices with their start and end apart: 31, of which 13 were waited for; matrix products, arithmetic and copies ran while one was open for 7% of the time, Pallas kernels for 0%

commit v1 on v0

--- a/solution.py
+++ b/solution.py
@@ -55,12 +55,15 @@
     flat = belief.reshape(K, -1)
     values = corrected.reshape(M, -1)
     count, first, squares = lax.psum(
-        (
-            jnp.sum(flat, axis=1),
-            jnp.dot(flat, values.T, precision=highest),
-            jnp.dot(flat, (values * values).T, precision=highest),
+        lax.psum(
+            (
+                jnp.sum(flat, axis=1),
+                jnp.dot(flat, values.T, precision=highest),
+                jnp.dot(flat, (values * values).T, precision=highest),
+            ),
+            ("row", "col"),
         ),
-        ("slab", "row", "col"),
+        "slab",
     )
     means = first / (count + 1.0)[:, None]
     spread = squares - 2.0 * means * first + means * means * count[:, None]

time: 242 us -> 212 us (0.88)
  blocking collectives: 80.2 us -> 50.2 us
    psum x2, blocking collectives: 68.3 us -> 16.3 us  [class_moments(): lax.psum((jnp.sum(flat, axis=1), jnp.dot(flat, values.T, precision=highes...]
    psum x0 -> x2, blocking collectives: none -> 22.1 us  [class_moments(): lax.psum(lax.psum((jnp.sum(flat, axis=1), jnp.dot(flat, values.T, precisi...]
  transfers between devices with their start and end apart: 31 -> 31, of which waited for: 13 -> 13; matrix products, arithmetic and copies ran while one was open for 7% -> 8% of each run, Pallas kernels for 0% -> 0%
where the time goes in v1:
time: 212 us; the launch traced here: 211 us
  starting transfers between devices  83.8 us (40%)
  blocking collectives  50.2 us (24%)
  local copies, waits for them, and re-layouts  26 us (12%)
  waiting for transfers between devices  25.4 us (12%)
  matrix products  12.9 us (6%)
  other arithmetic  9.55 us (5%)
  between operations  2.91 us (1%)
    ppermute x12, starting transfers between devices, extended(): lax.ppermute(tail, axis, [(i, (i + 1) % count) for i in range(ends)])  41.2 us
    psum x2, blocking collectives, class_moments(): lax.psum(lax.psum((jnp.sum(flat, axis=1), jnp.dot(flat, values.T, precisi...  22.1 us
    psum x2, blocking collectives, class_moments(): lax.psum((jnp.sum(flat, axis=1), jnp.dot(flat, values.T, precision=highes...  16.3 us
    ppermute x12, starting transfers between devices, extended(): lax.ppermute(head, axis, [((i + 1) % count, i) for i in range(ends)])  15.5 us
    ppermute x12, waiting for transfers between devices, extended(): lax.ppermute(head, axis, [((i + 1) % count, i) for i in range(ends)])  10.2 us
    all_to_all x2, starting transfers between devices, smoothed(): lax.all_to_all(mixed, 'slab', split_axis=1, concat_axis=2, tiled=True)  10.1 us
    slice x8, local copies, waits for them, and re-layouts, extended(): head = lax.slice_in_dim(cells, 0, width, axis=dim)  8.46 us
    all_to_all x1, blocking collectives, smoothed(): lax.all_to_all(across, 'row', split_axis=1, concat_axis=2, tiled=True)  7.42 us
  transfers between devices with their start and end apart: 31, of which 13 were waited for; matrix products, arithmetic and copies ran while one was open for 8% of the time, Pallas kernels for 0%

profile of v1, /device:TPU:0, one launch (start us, length us, event | category | flops | bytes accessed | tf_op | source)
XLA Modules:
  0.0 210.7 jit_solution(15308581820229277952)
XLA Ops:
  6.4 8.5 %all-reduce.1 = (f32[8,3]{0,1:T(4,128)S(1)}, f32[8,3]{0,1:T(4,128)S(1)}, f32[8]{0:T(128)S(1)}) all-reduce(f32[8,3]{0,1:T(4,128)S(1)} %fusion.2, f32[8,3]{0,1:T(4,128)S(1)} %convolution_bitcast_fusion.6, f32[8]{0:T(128)S(1)} %select_reduce_fusion), channel_id=1, replica_groups=mesh['grp'=2,'slab'=4,'row'=2,'col'=2] {'row','col'}, use_global_device_ids=true, to_apply=%region_7.8 | all-reduce | flops 56 | bytes 448 | tf_op jit(solution)/shard_map/psum | solution.py:58
  14.9 12.1 %all-reduce.3 = (f32[8,3]{0,1:T(4,128)S(1)}, f32[8,3]{0,1:T(4,128)S(1)}, f32[8]{0:T(128)S(1)}) all-reduce(f32[8,3]{0,1:T(4,128)S(1)} %get-tuple-element.14, f32[8,3]{0,1:T(4,128)S(1)} %get-tuple-element.15, f32[8]{0:T(128)S(1)} %get-tuple-element.16), channel_id=1, replica_groups=mesh['grp'=2,'slab'=4,'row'=2,'col'=2] {'slab'}, use_global_device_ids=true, to_apply=%region_8.9 | all-reduce | flops 56 | bytes 448 | tf_op jit(solution)/shard_map/psum | solution.py:57
  32.9 3.4 %all-to-all-start = ((f32[3,8,16,128]{3,2,0,1:T(8,128)}), f32[3,8,16,128]{3,2,0,1:T(8,128)S(1)}, u32[]{:S(2)}, u32[]{:S(2)}) async-start(f32[3,8,16,128]{3,2,0,1:T(8,128)} %fusion.39), calls=%async_computation | async-start | bytes 393216 | tf_op jit(solution)/shard_map/all_to_all | solution.py:92
  36.8 4.5 %all-to-all-done = f32[3,8,16,128]{3,2,0,1:T(8,128)S(1)} async-done(((f32[3,8,16,128]{3,2,0,1:T(8,128)}), f32[3,8,16,128]{3,2,0,1:T(8,128)S(1)}, u32[]{:S(2)}, u32[]{:S(2)}) %all-to-all-start) | async-done | bytes 196640 | tf_op jit(solution)/shard_map/all_to_all | solution.py:92
  42.5 3.4 %all-to-all-start.1 = ((f32[3,4,32,128]{3,1,0,2:T(4,128)}), f32[3,4,32,128]{3,1,0,2:T(4,128)S(1)}, u32[]{:S(2)}, u32[]{:S(2)}) async-start(f32[3,4,32,128]{3,1,0,2:T(4,128)} %copy.240), calls=%async_computation.1 | async-start | bytes 393216 | tf_op jit(solution)/shard_map/all_to_all | solution.py:96
  51.6 3.4 %all-to-all-start.2 = ((f32[3,8,16,128]{3,1,0,2:T(8,128)}), f32[3,8,16,128]{3,1,0,2:T(8,128)S(1)}, u32[]{:S(2)}, u32[]{:S(2)}) async-start(f32[3,8,16,128]{3,1,0,2:T(8,128)} %copy.243), calls=%async_computation.2 | async-start | bytes 393216 | tf_op jit(solution)/shard_map/all_to_all | solution.py:99
  56.3 4.5 %collective-permute-start.3 = (f32[8,10,1,128]{3,0,2,1:T(8,128)S(1)}, f32[8,10,1,128]{3,0,2,1:T(8,128)S(1)}, u32[]{:S(2)}, u32[]{:S(2)}) collective-permute-start(f32[8,10,1,128]{3,0,2,1:T(8,128)S(1)} %copy.339), channel_id=1, source_target_pairs={{0,2},{1,3},{4,6},{5,7},{8,10},{9,11},{12,14},{13,15},{16,18},{17,... | collective-permute-start | bytes 122888 | tf_op jit(solution)/shard_map/ppermute | solution.py:24
  64.0 5.0 %all-to-all-start.3 = ((f32[3,32,4,128]{3,2,0,1:T(4,128)}), f32[3,32,4,128]{3,2,0,1:T(4,128)S(1)}, u32[]{:S(2)}, u32[]{:S(2)}) async-start(f32[3,32,4,128]{3,2,0,1:T(4,128)} %copy.247), calls=%async_computation.3 | async-start | bytes 393216 | tf_op jit(solution)/shard_map/all_to_all | solution.py:103
  81.4 3.9 %collective-permute-start.7 = (f32[8,1,16,128]{3,2,1,0:T(8,128)S(1)}, f32[8,1,16,128]{3,2,1,0:T(8,128)S(1)}, u32[]{:S(2)}, u32[]{:S(2)}) collective-permute-start(f32[8,1,16,128]{3,2,1,0:T(8,128)S(1)} %get-tuple-element.59), channel_id=1, source_target_pairs={{0,4},{4,8},{8,12},{1,5},{5,9},{9,13},{2,6},{6,10},{10,14},{3,7},{... | collective-permute-start | bytes 196616 | tf_op jit(solution)/shard_map/ppermute | solution.py:24
  87.2 4.3 %collective-permute-done.6 = f32[8,1,16,128]{3,2,1,0:T(8,128)S(1)} collective-permute-done((f32[8,1,16,128]{3,2,1,0:T(8,128)S(1)}, f32[8,1,16,128]{3,2,1,0:T(8,128)S(1)}, u32[]{:S(2)}, u32[]{:S(2)}) %collective-permute-start.6) | collective-permute-done | bytes 65568 | tf_op jit(solution)/shard_map/ppermute | solution.py:26
  92.9 4.7 %collective-permute-start.9 = (f32[8,10,1,128]{3,0,2,1:T(8,128)S(1)}, f32[8,10,1,128]{3,0,2,1:T(8,128)S(1)}, u32[]{:S(2)}, u32[]{:S(2)}) collective-permute-start(f32[8,10,1,128]{3,0,2,1:T(8,128)S(1)} %copy.341), channel_id=1, source_target_pairs={{0,2},{1,3},{4,6},{5,7},{8,10},{9,11},{12,14},{13,15},{16,18},{17,... | collective-permute-start | bytes 122888 | tf_op jit(solution)/shard_map/ppermute | solution.py:24
  103.3 3.8 %collective-permute-start.11 = (f32[8,10,18,1]{2,0,3,1:T(8,128)S(1)}, f32[8,10,18,1]{2,0,3,1:T(8,128)}, u32[]{:S(2)}, u32[]{:S(2)}) collective-permute-start(f32[8,10,18,1]{2,0,3,1:T(8,128)S(1)} %copy.270), channel_id=1, source_target_pairs={{0,1},{2,3},{4,5},{6,7},{8,9},{10,11},{12,13},{14,15},{16,17},{18,... | collective-permute-start | bytes 17288 | tf_op jit(solution)/shard_map/ppermute | solution.py:24
  113.6 7.8 %all-reduce = (f32[8,3]{0,1:T(4,128)S(1)}, f32[8]{0:T(128)S(1)}, f32[8,3]{0,1:T(4,128)S(1)}) all-reduce(f32[8,3]{0,1:T(4,128)S(1)} %convolution_bitcast_fusion.5, f32[8]{0:T(128)S(1)} %get-tuple-element.10, f32[8,3]{0,1:T(4,128)S(1)} %convolution_bitcast_fusion.4), channel_id=1, replica_groups=mesh['grp'=2,'slab'=4,'row'=2,'col'=2] {'row','col'}, use_global_device_ids=true, to_apply=%region_19.20 | all-reduce | flops 56 | bytes 448 | tf_op jit(solution)/shard_map/psum | solution.py:58
  121.4 10.0 %all-reduce.2 = (f32[8,3]{0,1:T(4,128)S(1)}, f32[8]{0:T(128)S(1)}, f32[8,3]{0,1:T(4,128)S(1)}) all-reduce(f32[8,3]{0,1:T(4,128)S(1)} %get-tuple-element.11, f32[8]{0:T(128)S(1)} %get-tuple-element.12, f32[8,3]{0,1:T(4,128)S(1)} %get-tuple-element.13), channel_id=1, replica_groups=mesh['grp'=2,'slab'=4,'row'=2,'col'=2] {'slab'}, use_global_device_ids=true, to_apply=%region_20.21 | all-reduce | flops 56 | bytes 448 | tf_op jit(solution)/shard_map/psum | solution.py:57
  136.4 7.4 %all_to_all.144 = f32[3,8,16,128]{3,2,0,1:T(8,128)S(1)} all-to-all(f32[3,8,16,128]{3,2,0,1:T(8,128)S(1)} %fusion.37), channel_id=1, replica_groups=mesh['grp'=2,'slab'=4,'row'=2,'col'=2] {'row'}, dimensions={1} | all-to-all | bytes 393216 | tf_op jit(solution)/shard_map/all_to_all | solution.py:92
  145.0 3.4 %all-to-all-start.5 = ((f32[3,4,32,128]{3,1,0,2:T(4,128)}), f32[3,4,32,128]{3,1,0,2:T(4,128)S(1)}, u32[]{:S(2)}, u32[]{:S(2)}) async-start(f32[3,4,32,128]{3,1,0,2:T(4,128)} %copy.281), calls=%async_computation.5 | async-start | bytes 393216 | tf_op jit(solution)/shard_map/all_to_all | solution.py:96
  154.1 3.4 %all-to-all-start.6 = ((f32[3,8,16,128]{3,1,0,2:T(8,128)}), f32[3,8,16,128]{3,1,0,2:T(8,128)S(1)}, u32[]{:S(2)}, u32[]{:S(2)}) async-start(f32[3,8,16,128]{3,1,0,2:T(8,128)} %copy.284), calls=%async_computation.6 | async-start | bytes 393216 | tf_op jit(solution)/shard_map/all_to_all | solution.py:99
  158.8 4.5 %collective-permute-start.15 = (f32[8,10,1,128]{3,0,2,1:T(8,128)S(1)}, f32[8,10,1,128]{3,0,2,1:T(8,128)S(1)}, u32[]{:S(2)}, u32[]{:S(2)}) collective-permute-start(f32[8,10,1,128]{3,0,2,1:T(8,128)S(1)} %copy.343), channel_id=1, source_target_pairs={{0,2},{1,3},{4,6},{5,7},{8,10},{9,11},{12,14},{13,15},{16,18},{17,... | collective-permute-start | bytes 122888 | tf_op jit(solution)/shard_map/ppermute | solution.py:24
  166.5 5.0 %all-to-all-start.7 = ((f32[3,32,4,128]{3,2,0,1:T(4,128)}), f32[3,32,4,128]{3,2,0,1:T(4,128)S(1)}, u32[]{:S(2)}, u32[]{:S(2)}) async-start(f32[3,32,4,128]{3,2,0,1:T(4,128)} %copy.288), calls=%async_computation.7 | async-start | bytes 393216 | tf_op jit(solution)/shard_map/all_to_all | solution.py:103
  176.4 3.0 %collective-permute-start.17 = (f32[8,10,18,1]{2,0,3,1:T(8,128)S(1)}, f32[8,10,18,1]{2,0,3,1:T(8,128)S(1)}, u32[]{:S(2)}, u32[]{:S(2)}) collective-permute-start(f32[8,10,18,1]{2,0,3,1:T(8,128)S(1)} %copy.303), channel_id=1, source_target_pairs={{0,1},{2,3},{4,5},{6,7},{8,9},{10,11},{12,13},{14,15},{16,17},{18,... | collective-permute-start | bytes 17288 | tf_op jit(solution)/shard_map/ppermute | solution.py:24
  184.0 3.9 %collective-permute-start.19 = (f32[8,1,16,128]{3,2,1,0:T(8,128)S(1)}, f32[8,1,16,128]{3,2,1,0:T(8,128)S(1)}, u32[]{:S(2)}, u32[]{:S(2)}) collective-permute-start(f32[8,1,16,128]{3,2,1,0:T(8,128)S(1)} %get-tuple-element.55), channel_id=1, source_target_pairs={{0,4},{4,8},{8,12},{1,5},{5,9},{9,13},{2,6},{6,10},{10,14},{3,7},{... | collective-permute-start | bytes 196616 | tf_op jit(solution)/shard_map/ppermute | solution.py:24
  189.8 4.3 %collective-permute-done.18 = f32[8,1,16,128]{3,2,1,0:T(8,128)S(1)} collective-permute-done((f32[8,1,16,128]{3,2,1,0:T(8,128)S(1)}, f32[8,1,16,128]{3,2,1,0:T(8,128)S(1)}, u32[]{:S(2)}, u32[]{:S(2)}) %collective-permute-start.18) | collective-permute-done | bytes 65568 | tf_op jit(solution)/shard_map/ppermute | solution.py:26
  195.5 4.8 %collective-permute-start.21 = (f32[8,10,1,128]{3,0,2,1:T(8,128)S(1)}, f32[8,10,1,128]{3,0,2,1:T(8,128)S(1)}, u32[]{:S(2)}, u32[]{:S(2)}) collective-permute-start(f32[8,10,1,128]{3,0,2,1:T(8,128)S(1)} %copy.345), channel_id=1, source_target_pairs={{0,2},{1,3},{4,6},{5,7},{8,10},{9,11},{12,14},{13,15},{16,18},{17,... | collective-permute-start | bytes 122888 | tf_op jit(solution)/shard_map/ppermute | solution.py:24
  204.7 3.0 %collective-permute-start.23 = (f32[8,10,18,1]{2,0,3,1:T(8,128)S(1)}, f32[8,10,18,1]{2,0,3,1:T(8,128)S(1)}, u32[]{:S(2)}, u32[]{:S(2)}) collective-permute-start(f32[8,10,18,1]{2,0,3,1:T(8,128)S(1)} %copy.313), channel_id=1, source_target_pairs={{0,1},{2,3},{4,5},{6,7},{8,9},{10,11},{12,13},{14,15},{16,17},{18,... | collective-permute-start | bytes 17288 | tf_op jit(solution)/shard_map/ppermute | solution.py:24
  (196 shorter events, 85.6 us)
Async XLA Ops:
  32.9 8.5 %all-to-all-start = ((f32[3,8,16,128]{3,2,0,1:T(8,128)}), f32[3,8,16,128]{3,2,0,1:T(8,128)S(1)}, u32[]{:S(2)}, u32[]{:S(2)}) async-start(f32[3,8,16,128]{3,2,0,1:T(8,128)} %fusion.39), calls=%async_computation | async-start | bytes 393216 | tf_op jit(solution)/shard_map/all_to_all | solution.py:92
  42.5 8.2 %all-to-all-start.1 = ((f32[3,4,32,128]{3,1,0,2:T(4,128)}), f32[3,4,32,128]{3,1,0,2:T(4,128)S(1)}, u32[]{:S(2)}, u32[]{:S(2)}) async-start(f32[3,4,32,128]{3,1,0,2:T(4,128)} %copy.240), calls=%async_computation.1 | async-start | bytes 393216 | tf_op jit(solution)/shard_map/all_to_all | solution.py:96
  46.0 8.9 %collective-permute-start.1 = (f32[8,1,16,128]{3,2,1,0:T(8,128)S(1)}, f32[8,1,16,128]{3,2,1,0:T(8,128)S(1)}, u32[]{:S(2)}, u32[]{:S(2)}) collective-permute-start(f32[8,1,16,128]{3,2,1,0:T(8,128)S(1)} %get-tuple-element.61), channel_id=1, source_target_pairs={{0,4},{4,8},{8,12},{1,5},{5,9},{9,13},{2,6},{6,10},{10,14},{3,7},{... | collective-permute-start | bytes 196616 | tf_op jit(solution)/shard_map/ppermute | solution.py:24
  47.3 7.7 %collective-permute-start = (f32[8,1,16,128]{3,2,1,0:T(8,128)S(1)}, f32[8,1,16,128]{3,2,1,0:T(8,128)S(1)}, u32[]{:S(2)}, u32[]{:S(2)}) collective-permute-start(f32[8,1,16,128]{3,2,1,0:T(8,128)S(1)} %get-tuple-element.62), channel_id=1, source_target_pairs={{4,0},{8,4},{12,8},{5,1},{9,5},{13,9},{6,2},{10,6},{14,10},{7,3},{... | collective-permute-start | bytes 196616 | tf_op jit(solution)/shard_map/ppermute | solution.py:26
  51.6 11.2 %all-to-all-start.2 = ((f32[3,8,16,128]{3,1,0,2:T(8,128)}), f32[3,8,16,128]{3,1,0,2:T(8,128)S(1)}, u32[]{:S(2)}, u32[]{:S(2)}) async-start(f32[3,8,16,128]{3,1,0,2:T(8,128)} %copy.243), calls=%async_computation.2 | async-start | bytes 393216 | tf_op jit(solution)/shard_map/all_to_all | solution.py:99
  55.0 5.9 %collective-permute-start.2 = (f32[8,10,1,128]{3,0,2,1:T(8,128)S(1)}, f32[8,10,1,128]{3,0,2,1:T(8,128)S(1)}, u32[]{:S(2)}, u32[]{:S(2)}) collective-permute-start(f32[8,10,1,128]{3,0,2,1:T(8,128)S(1)} %copy.338), channel_id=1, source_target_pairs={{2,0},{3,1},{6,4},{7,5},{10,8},{11,9},{14,12},{15,13},{18,16},{19,... | collective-permute-start | bytes 122888 | tf_op jit(solution)/shard_map/ppermute | solution.py:26
  56.3 6.2 %collective-permute-start.3 = (f32[8,10,1,128]{3,0,2,1:T(8,128)S(1)}, f32[8,10,1,128]{3,0,2,1:T(8,128)S(1)}, u32[]{:S(2)}, u32[]{:S(2)}) collective-permute-start(f32[8,10,1,128]{3,0,2,1:T(8,128)S(1)} %copy.339), channel_id=1, source_target_pairs={{0,2},{1,3},{4,6},{5,7},{8,10},{9,11},{12,14},{13,15},{16,18},{17,... | collective-permute-start | bytes 122888 | tf_op jit(solution)/shard_map/ppermute | solution.py:24
  64.0 15.2 %all-to-all-start.3 = ((f32[3,32,4,128]{3,2,0,1:T(4,128)}), f32[3,32,4,128]{3,2,0,1:T(4,128)S(1)}, u32[]{:S(2)}, u32[]{:S(2)}) async-start(f32[3,32,4,128]{3,2,0,1:T(4,128)} %copy.247), calls=%async_computation.3 | async-start | bytes 393216 | tf_op jit(solution)/shard_map/all_to_all | solution.py:103
  81.4 5.8 %collective-permute-start.7 = (f32[8,1,16,128]{3,2,1,0:T(8,128)S(1)}, f32[8,1,16,128]{3,2,1,0:T(8,128)S(1)}, u32[]{:S(2)}, u32[]{:S(2)}) collective-permute-start(f32[8,1,16,128]{3,2,1,0:T(8,128)S(1)} %get-tuple-element.59), channel_id=1, source_target_pairs={{0,4},{4,8},{8,12},{1,5},{5,9},{9,13},{2,6},{6,10},{10,14},{3,7},{... | collective-permute-start | bytes 196616 | tf_op jit(solution)/shard_map/ppermute | solution.py:24
  85.3 6.2 %collective-permute-start.6 = (f32[8,1,16,128]{3,2,1,0:T(8,128)S(1)}, f32[8,1,16,128]{3,2,1,0:T(8,128)S(1)}, u32[]{:S(2)}, u32[]{:S(2)}) collective-permute-start(f32[8,1,16,128]{3,2,1,0:T(8,128)S(1)} %get-tuple-element.60), channel_id=1, source_target_pairs={{4,0},{8,4},{12,8},{5,1},{9,5},{13,9},{6,2},{10,6},{14,10},{7,3},{... | collective-permute-start | bytes 196616 | tf_op jit(solution)/shard_map/ppermute | solution.py:26
  91.5 6.0 %collective-permute-start.8 = (f32[8,10,1,128]{3,0,2,1:T(8,128)S(1)}, f32[8,10,1,128]{3,0,2,1:T(8,128)S(1)}, u32[]{:S(2)}, u32[]{:S(2)}) collective-permute-start(f32[8,10,1,128]{3,0,2,1:T(8,128)S(1)} %copy.340), channel_id=1, source_target_pairs={{2,0},{3,1},{6,4},{7,5},{10,8},{11,9},{14,12},{15,13},{18,16},{19,... | collective-permute-start | bytes 122888 | tf_op jit(solution)/shard_map/ppermute | solution.py:26
  92.9 6.2 %collective-permute-start.9 = (f32[8,10,1,128]{3,0,2,1:T(8,128)S(1)}, f32[8,10,1,128]{3,0,2,1:T(8,128)S(1)}, u32[]{:S(2)}, u32[]{:S(2)}) collective-permute-start(f32[8,10,1,128]{3,0,2,1:T(8,128)S(1)} %copy.341), channel_id=1, source_target_pairs={{0,2},{1,3},{4,6},{5,7},{8,10},{9,11},{12,14},{13,15},{16,18},{17,... | collective-permute-start | bytes 122888 | tf_op jit(solution)/shard_map/ppermute | solution.py:24
  101.4 5.6 %collective-permute-start.10 = (f32[8,10,18,1]{2,0,3,1:T(8,128)}, f32[8,10,18,1]{2,0,3,1:T(8,128)S(1)}, u32[]{:S(2)}, u32[]{:S(2)}) collective-permute-start(f32[8,10,18,1]{2,0,3,1:T(8,128)} %copy.268), channel_id=1, source_target_pairs={{1,0},{3,2},{5,4},{7,6},{9,8},{11,10},{13,12},{15,14},{17,16},{19,... | collective-permute-start | bytes 17288 | tf_op jit(solution)/shard_map/ppermute | solution.py:26
  145.0 8.2 %all-to-all-start.5 = ((f32[3,4,32,128]{3,1,0,2:T(4,128)}), f32[3,4,32,128]{3,1,0,2:T(4,128)S(1)}, u32[]{:S(2)}, u32[]{:S(2)}) async-start(f32[3,4,32,128]{3,1,0,2:T(4,128)} %copy.281), calls=%async_computation.5 | async-start | bytes 393216 | tf_op jit(solution)/shard_map/all_to_all | solution.py:96
  148.5 8.9 %collective-permute-start.13 = (f32[8,1,16,128]{3,2,1,0:T(8,128)S(1)}, f32[8,1,16,128]{3,2,1,0:T(8,128)S(1)}, u32[]{:S(2)}, u32[]{:S(2)}) collective-permute-start(f32[8,1,16,128]{3,2,1,0:T(8,128)S(1)} %get-tuple-element.57), channel_id=1, source_target_pairs={{0,4},{4,8},{8,12},{1,5},{5,9},{9,13},{2,6},{6,10},{10,14},{3,7},{... | collective-permute-start | bytes 196616 | tf_op jit(solution)/shard_map/ppermute | solution.py:24
  150.9 6.6 %collective-permute-start.12 = (f32[8,1,16,128]{3,2,1,0:T(8,128)S(1)}, f32[8,1,16,128]{3,2,1,0:T(8,128)S(1)}, u32[]{:S(2)}, u32[]{:S(2)}) collective-permute-start(f32[8,1,16,128]{3,2,1,0:T(8,128)S(1)} %get-tuple-element.58), channel_id=1, source_target_pairs={{4,0},{8,4},{12,8},{5,1},{9,5},{13,9},{6,2},{10,6},{14,10},{7,3},{... | collective-permute-start | bytes 196616 | tf_op jit(solution)/shard_map/ppermute | solution.py:26
  154.1 11.2 %all-to-all-start.6 = ((f32[3,8,16,128]{3,1,0,2:T(8,128)}), f32[3,8,16,128]{3,1,0,2:T(8,128)S(1)}, u32[]{:S(2)}, u32[]{:S(2)}) async-start(f32[3,8,16,128]{3,1,0,2:T(8,128)} %copy.284), calls=%async_computation.6 | async-start | bytes 393216 | tf_op jit(solution)/shard_map/all_to_all | solution.py:99
  157.5 5.9 %collective-permute-start.14 = (f32[8,10,1,128]{3,0,2,1:T(8,128)S(1)}, f32[8,10,1,128]{3,0,2,1:T(8,128)S(1)}, u32[]{:S(2)}, u32[]{:S(2)}) collective-permute-start(f32[8,10,1,128]{3,0,2,1:T(8,128)S(1)} %copy.342), channel_id=1, source_target_pairs={{2,0},{3,1},{6,4},{7,5},{10,8},{11,9},{14,12},{15,13},{18,16},{19,... | collective-permute-start | bytes 122888 | tf_op jit(solution)/shard_map/ppermute | solution.py:26
  158.8 6.2 %collective-permute-start.15 = (f32[8,10,1,128]{3,0,2,1:T(8,128)S(1)}, f32[8,10,1,128]{3,0,2,1:T(8,128)S(1)}, u32[]{:S(2)}, u32[]{:S(2)}) collective-permute-start(f32[8,10,1,128]{3,0,2,1:T(8,128)S(1)} %copy.343), channel_id=1, source_target_pairs={{0,2},{1,3},{4,6},{5,7},{8,10},{9,11},{12,14},{13,15},{16,18},{17,... | collective-permute-start | bytes 122888 | tf_op jit(solution)/shard_map/ppermute | solution.py:24
  166.5 15.4 %all-to-all-start.7 = ((f32[3,32,4,128]{3,2,0,1:T(4,128)}), f32[3,32,4,128]{3,2,0,1:T(4,128)S(1)}, u32[]{:S(2)}, u32[]{:S(2)}) async-start(f32[3,32,4,128]{3,2,0,1:T(4,128)} %copy.288), calls=%async_computation.7 | async-start | bytes 393216 | tf_op jit(solution)/shard_map/all_to_all | solution.py:103
  184.0 5.8 %collective-permute-start.19 = (f32[8,1,16,128]{3,2,1,0:T(8,128)S(1)}, f32[8,1,16,128]{3,2,1,0:T(8,128)S(1)}, u32[]{:S(2)}, u32[]{:S(2)}) collective-permute-start(f32[8,1,16,128]{3,2,1,0:T(8,128)S(1)} %get-tuple-element.55), channel_id=1, source_target_pairs={{0,4},{4,8},{8,12},{1,5},{5,9},{9,13},{2,6},{6,10},{10,14},{3,7},{... | collective-permute-start | bytes 196616 | tf_op jit(solution)/shard_map/ppermute | solution.py:24
  188.0 6.2 %collective-permute-start.18 = (f32[8,1,16,128]{3,2,1,0:T(8,128)S(1)}, f32[8,1,16,128]{3,2,1,0:T(8,128)S(1)}, u32[]{:S(2)}, u32[]{:S(2)}) collective-permute-start(f32[8,1,16,128]{3,2,1,0:T(8,128)S(1)} %get-tuple-element.56), channel_id=1, source_target_pairs={{4,0},{8,4},{12,8},{5,1},{9,5},{13,9},{6,2},{10,6},{14,10},{7,3},{... | collective-permute-start | bytes 196616 | tf_op jit(solution)/shard_map/ppermute | solution.py:26
  194.2 6.1 %collective-permute-start.20 = (f32[8,10,1,128]{3,0,2,1:T(8,128)S(1)}, f32[8,10,1,128]{3,0,2,1:T(8,128)S(1)}, u32[]{:S(2)}, u32[]{:S(2)}) collective-permute-start(f32[8,10,1,128]{3,0,2,1:T(8,128)S(1)} %copy.344), channel_id=1, source_target_pairs={{2,0},{3,1},{6,4},{7,5},{10,8},{11,9},{14,12},{15,13},{18,16},{19,... | collective-permute-start | bytes 122888 | tf_op jit(solution)/shard_map/ppermute | solution.py:26
  195.5 6.2 %collective-permute-start.21 = (f32[8,10,1,128]{3,0,2,1:T(8,128)S(1)}, f32[8,10,1,128]{3,0,2,1:T(8,128)S(1)}, u32[]{:S(2)}, u32[]{:S(2)}) collective-permute-start(f32[8,10,1,128]{3,0,2,1:T(8,128)S(1)} %copy.345), channel_id=1, source_target_pairs={{0,2},{1,3},{4,6},{5,7},{8,10},{9,11},{12,14},{13,15},{16,18},{17,... | collective-permute-start | bytes 122888 | tf_op jit(solution)/shard_map/ppermute | solution.py:24
  (26 other events, 201.5 us)
